TPU v7x, 256 devices: a 8x8x2 block of a 8x8x16 slice. The times are simulated.
256 devices in a mesh: groups: 2 (over z), seq: 128 (over y, x, core).
Axes of the slice: x: 8, y: 8, z: 2, core: 2. Of those that a mesh axis runs over, the one named last changes fastest.
The devices are a block of a 8x8x16 slice.
Arguments:
- queries: bfloat16 [8192, 2048], P(('groups', 'seq')), parts along dimension 0, may hold values from -132 to 132
- fresh_keys: bfloat16 [8192, 2048], P(('groups', 'seq')), parts along dimension 0, may hold values from -6 to 6
- fresh_values: bfloat16 [8192, 2048], P(('groups', 'seq')), parts along dimension 0, may hold values from -48 to 48
- stale_keys: bfloat16 [8192, 2048], P(('groups', 'seq')), parts along dimension 0, may hold values from -6 to 6
- stale_values: bfloat16 [8192, 2048], P(('groups', 'seq')), parts along dimension 0, may hold values from -48 to 48
- patch_sizes: int32 [8], P('groups'), parts along dimension 0, may hold values from 1 to 2048, 4096 in all
Outputs:
- attended: bfloat16 [8192, 2048], P(('groups', 'seq')), parts along dimension 0
There are 2 independent parts, one for each index of `groups`. A program takes and returns all parts, laid end to end along the dimension named above; each array names one. Nothing has to cross between parts.
Inputs may be any that keep to these rules, and one draw needn't show every extreme that they name: `patch_sizes`: the patch lengths sum to 4096.
All inputs are finite; a program needn't handle non-finite values.
Results may differ from a plain program's by a relative error of at most 0.006.
Values may be sent and summed in bfloat16 or wider, within the bound.
A program may use at most 64 MiB of HBM per device.

v0:
```python
import jax
import jax.numpy as jnp
from jax import lax
from jax.sharding import PartitionSpec as P

H = 16


def in_one_piece(arrays, axis, split_dim, concat_dim, along):
    ends, at = ([], 0)
    for a in arrays[:-1]:
        at += a.shape[along]
        ends.append(at)
    both = jnp.concatenate(arrays, axis=along)
    return tuple(
        jnp.split(
            lax.all_to_all(both, axis, split_axis=split_dim, concat_axis=concat_dim, tiled=True),
            ends,
            axis=along,
        )
    )


def shifted(block, axis, distance):
    devices = range(lax.axis_size(axis))
    route = [((i - distance) % len(devices), i) for i in devices]
    return lax.ppermute(block, axis, route)


def shards(queries, fresh_keys, fresh_values, stale_keys, stale_values, patch_sizes):
    local_rows, columns = queries.shape
    head_size = columns // H
    devices = lax.axis_size("seq")
    query_groups = devices // H
    sub_rows = local_rows // query_groups
    shape_in = (sub_rows, devices, head_size)
    moved = in_one_piece(
        (
            queries.reshape(shape_in),
            fresh_keys.reshape(shape_in),
            fresh_values.reshape(shape_in),
            stale_keys.reshape(shape_in),
            stale_values.reshape(shape_in),
        ),
        "seq",
        1,
        0,
        2,
    )
    query_rows = moved[0].reshape(-1, head_size)
    stacked = jnp.stack(
        [
            moved[1].reshape(-1, head_size),
            moved[2].reshape(-1, head_size),
            moved[3].reshape(-1, head_size),
            moved[4].reshape(-1, head_size),
        ]
    )
    own_group = lax.axis_index("seq") // H
    patch_ends = jnp.cumsum(patch_sizes)[:-1]
    positions = (
        jnp.arange(devices, dtype=jnp.int32)[:, None] * local_rows
        + jnp.arange(sub_rows, dtype=jnp.int32)[None, :] * query_groups
    ).reshape(-1)

    def patch_of(group):
        hits = positions[:, None] + group >= patch_ends[None, :]
        return jnp.sum(hits.astype(jnp.int32), axis=1)

    score_scale = head_size ** (-0.5)
    contract = (((1,), (1,)), ((), ()))
    query_patch = patch_of(own_group)

    def absorb(carry_state, key_block, source_group):
        running_max, denominator, numerator = carry_state
        is_fresh = patch_of(source_group)[None, :] <= query_patch[:, None]
        fresh_scores = lax.dot_general(
            query_rows, key_block[0], contract, preferred_element_type=jnp.float32
        )
        stale_scores = lax.dot_general(
            query_rows, key_block[2], contract, preferred_element_type=jnp.float32
        )
        scores = jnp.where(is_fresh, fresh_scores, stale_scores) * score_scale
        new_max = jnp.maximum(running_max, jnp.max(scores, axis=1, keepdims=True))
        rescale = jnp.exp(running_max - new_max)
        weights = jnp.exp(scores - new_max)
        denominator = denominator * rescale + jnp.sum(weights, axis=1, keepdims=True)
        rounded = weights.astype(jnp.bfloat16)
        zeroes = jnp.zeros_like(rounded)
        numerator = numerator * rescale + jnp.dot(
            jnp.where(is_fresh, rounded, zeroes), key_block[1], preferred_element_type=jnp.float32
        )
        numerator = numerator + jnp.dot(
            jnp.where(is_fresh, zeroes, rounded), key_block[3], preferred_element_type=jnp.float32
        )
        return (new_max, denominator, numerator)

    query_count = query_rows.shape[0]
    carry_state = (
        jnp.full((query_count, 1), -1e30, jnp.float32),
        jnp.zeros((query_count, 1), jnp.float32),
        jnp.zeros((query_count, head_size), jnp.float32),
    )
    carry_state = absorb(carry_state, stacked, own_group)
    forward = stacked
    backward = stacked
    for offset in range(1, query_groups // 2 + 1):
        forward = shifted(forward, "seq", H)
        if offset < query_groups - query_groups // 2:
            backward = shifted(backward, "seq", -H)
        carry_state = absorb(carry_state, forward, (own_group - offset) % query_groups)
        if offset < query_groups - query_groups // 2:
            carry_state = absorb(carry_state, backward, (own_group + offset) % query_groups)
    attended = (carry_state[2] / carry_state[1]).astype(jnp.bfloat16)
    returned = lax.all_to_all(
        attended.reshape(devices, sub_rows, 1, head_size),
        "seq",
        split_axis=0,
        concat_axis=2,
        tiled=True,
    )
    return returned.reshape(local_rows, columns)


def solution(mesh):
    in_specs = (
        P(("groups", "seq"), None),
        P(("groups", "seq"), None),
        P(("groups", "seq"), None),
        P(("groups", "seq"), None),
        P(("groups", "seq"), None),
        P("groups"),
    )
    out_specs = P(("groups", "seq"), None)
    return jax.shard_map(shards, mesh=mesh, in_specs=in_specs, out_specs=out_specs, check_vma=False)
```

profile of v0, /device:TPU:513, one launch (start us, length us, event | category | flops | bytes accessed | tf_op | source)
XLA Modules:
  0.0 146.3 jit_solution(11399076000162151006)
XLA Ops:
  0.0 1.0 reshape.416
  1.1 0.8 copy-done.1
  2.0 0.8 copy-done.2
  2.9 0.8 copy-done.3
  3.8 0.8 copy_dynamic-update-slice_fusion.4
  4.6 0.8 copy_dynamic-update-slice_fusion.3
  5.3 0.8 copy_dynamic-update-slice_fusion.2
  6.1 0.8 copy_dynamic-update-slice_fusion.1
  6.9 0.8 copy_dynamic-update-slice_fusion
  7.7 27.4 %all-to-all-start = ((bf16[4,128,640]{2,0,1:T(4,128)(2,1)}), bf16[4,128,640]{2,0,1:T(4,128)(2,1)S(1)}, u32[]{:S(2)}, u32[]{:S(2)}) async-start(bf16[4,128,640]{2,0,1:T(4,128)(2,1)} %copy_dynamic-update-slice_fusion), calls=%async_computation | async-start | bytes 1310720 | tf_op jit(solution)/shard_map/all_to_all | solution.py:17
  35.3 0.6 copy-done.4
  35.9 0.2 reduce-window.4
  36.3 0.1 add.401
  36.4 0.1 add.395
  36.5 0.1 add.388
  37.1 0.1 convert_reduce_fusion.1
  37.2 20.6 %all-to-all-done = bf16[4,128,640]{2,0,1:T(4,128)(2,1)S(1)} async-done(((bf16[4,128,640]{2,0,1:T(4,128)(2,1)}), bf16[4,128,640]{2,0,1:T(4,128)(2,1)S(1)}, u32[]{:S(2)}, u32[]{:S(2)}) %all-to-all-start) | async-done | bytes 655392 | tf_op jit(solution)/shard_map/all_to_all | solution.py:17
  57.8 0.1 all_to_all.27
  58.1 1.0 collective-permute-start.1
  59.1 0.6 collective-permute-start
  59.7 0.3 fusion.127
  60.0 0.3 fusion.159
  60.3 13.9 %collective-permute-done = bf16[4,512,128]{2,1,0:T(8,128)(2,1)S(1)} collective-permute-done((bf16[4,512,128]{2,1,0:T(8,128)(2,1)S(1)}, bf16[4,512,128]{2,1,0:T(8,128)(2,1)S(1)}, u32[]{:S(2)}, u32[]{:S(2)}) %collective-permute-start) | collective-permute-done | bytes 524320 | tf_op jit(solution)/shard_map/ppermute | solution.py:27
  74.2 0.3 fusion.123
  74.5 2.8 %collective-permute-start.3 = (bf16[4,512,128]{2,1,0:T(8,128)(2,1)S(1)}, bf16[4,512,128]{2,1,0:T(8,128)(2,1)S(1)}, u32[]{:S(2)}, u32[]{:S(2)}) collective-permute-start(bf16[4,512,128]{2,1,0:T(8,128)(2,1)S(1)} %collective-permute-done.1), channel_id=1, source_target_pairs={{16,0},{17,1},{18,2},{19,3},{20,4},{21,5},{22,6},{23,7},{24,8},{25... | collective-permute-start | bytes 1572872 | tf_op jit(solution)/shard_map/ppermute | solution.py:27
  77.3 0.3 fusion.158
  77.6 0.3 fusion.122
  77.9 0.3 fusion.157
  78.2 10.2 %collective-permute-done.2 = bf16[4,512,128]{2,1,0:T(8,128)(2,1)S(1)} collective-permute-done((bf16[4,512,128]{2,1,0:T(8,128)(2,1)S(1)}, bf16[4,512,128]{2,1,0:T(8,128)(2,1)S(1)}, u32[]{:S(2)}, u32[]{:S(2)}) %collective-permute-start.2) | collective-permute-done | bytes 524320 | tf_op jit(solution)/shard_map/ppermute | solution.py:27
  88.4 0.3 fusion.121
  88.8 3.0 %collective-permute-start.5 = (bf16[4,512,128]{2,1,0:T(8,128)(2,1)S(1)}, bf16[4,512,128]{2,1,0:T(8,128)(2,1)S(1)}, u32[]{:S(2)}, u32[]{:S(2)}) collective-permute-start(bf16[4,512,128]{2,1,0:T(8,128)(2,1)S(1)} %collective-permute-done.3), channel_id=1, source_target_pairs={{16,0},{17,1},{18,2},{19,3},{20,4},{21,5},{22,6},{23,7},{24,8},{25... | collective-permute-start | bytes 1572872 | tf_op jit(solution)/shard_map/ppermute | solution.py:27
  91.7 0.3 fusion.156
  92.0 0.3 fusion.120
  92.3 0.3 fusion.155
  92.7 9.2 %collective-permute-done.4 = bf16[4,512,128]{2,1,0:T(8,128)(2,1)S(1)} collective-permute-done((bf16[4,512,128]{2,1,0:T(8,128)(2,1)S(1)}, bf16[4,512,128]{2,1,0:T(8,128)(2,1)S(1)}, u32[]{:S(2)}, u32[]{:S(2)}) %collective-permute-start.4) | collective-permute-done | bytes 524320 | tf_op jit(solution)/shard_map/ppermute | solution.py:27
  101.8 0.3 fusion.119
  102.1 0.3 fusion.154
  102.5 0.3 fusion.118
  102.8 0.3 fusion.153
  103.1 11.3 %collective-permute-done.6 = bf16[4,512,128]{2,1,0:T(8,128)(2,1)S(1)} collective-permute-done((bf16[4,512,128]{2,1,0:T(8,128)(2,1)S(1)}, bf16[4,512,128]{2,1,0:T(8,128)(2,1)S(1)}, u32[]{:S(2)}, u32[]{:S(2)}) %collective-permute-start.6) | collective-permute-done | bytes 524320 | tf_op jit(solution)/shard_map/ppermute | solution.py:27
  114.3 0.3 fusion.117
  114.6 0.3 fusion.152
  115.0 0.3 fusion.27
  115.3 0.3 fusion.39
  115.6 0.3 fusion.35
  115.9 0.3 fusion.31
  116.2 0.4 convolution_add_fusion.5
  116.7 0.4 fusion.8
  117.1 0.4 fusion.52
  117.6 0.4 fusion.51
  118.0 0.4 fusion.50
  118.4 0.4 fusion.49
  118.9 0.4 fusion.48
  119.3 0.4 fusion.47
  119.8 0.4 fusion.46
  120.2 0.4 fusion.45
  120.7 0.4 fusion.44
  121.1 0.4 fusion.43
  121.5 0.5 fusion.25
  122.0 0.5 fusion.21
  122.5 0.5 fusion.17
  122.9 0.5 fusion.26
  123.4 22.1 %all_to_all.33 = bf16[128,4,1,128]{3,1,2,0:T(4,128)(2,1)S(1)} all-to-all(bf16[128,4,1,128]{3,1,2,0:T(4,128)(2,1)S(1)} %bitcast.174), channel_id=1, replica_groups=mesh['groups'=2,'seq'=128] {'seq'}, dimensions={0} | all-to-all | bytes 262144 | tf_op jit(solution)/shard_map/all_to_all | solution.py:115
  145.6 0.7 reshape.423
  (30 shorter events, 1.2 us)
Async XLA Ops:
  0.0 1.0 copy-start
  1.0 0.9 copy-start.1
  1.9 0.9 copy-start.2
  2.8 0.9 copy-start.3
  7.7 50.1 %all-to-all-start = ((bf16[4,128,640]{2,0,1:T(4,128)(2,1)}), bf16[4,128,640]{2,0,1:T(4,128)(2,1)S(1)}, u32[]{:S(2)}, u32[]{:S(2)}) async-start(bf16[4,128,640]{2,0,1:T(4,128)(2,1)} %copy_dynamic-update-slice_fusion), calls=%async_computation | async-start | bytes 1310720 | tf_op jit(solution)/shard_map/all_to_all | solution.py:17
  35.3 0.7 copy-start.4
  58.1 16.4 %collective-permute-start.1 = (bf16[4,512,128]{2,1,0:T(8,128)(2,1)S(1)}, bf16[4,512,128]{2,1,0:T(8,128)(2,1)S(1)}, u32[]{:S(2)}, u32[]{:S(2)}) collective-permute-start(bf16[4,512,128]{2,1,0:T(8,128)(2,1)S(1)} %pad_maximum_fusion), channel_id=1, source_target_pairs={{16,0},{17,1},{18,2},{19,3},{20,4},{21,5},{22,6},{23,7},{24,8},{25... | collective-permute-start | bytes 1572872 | tf_op jit(solution)/shard_map/ppermute | solution.py:27
  59.1 15.1 %collective-permute-start = (bf16[4,512,128]{2,1,0:T(8,128)(2,1)S(1)}, bf16[4,512,128]{2,1,0:T(8,128)(2,1)S(1)}, u32[]{:S(2)}, u32[]{:S(2)}) collective-permute-start(bf16[4,512,128]{2,1,0:T(8,128)(2,1)S(1)} %pad_maximum_fusion), channel_id=1, source_target_pairs={{112,0},{113,1},{114,2},{115,3},{116,4},{117,5},{118,6},{119,7},{1... | collective-permute-start | bytes 1572872 | tf_op jit(solution)/shard_map/ppermute | solution.py:27
  74.2 14.2 %collective-permute-start.2 = (bf16[4,512,128]{2,1,0:T(8,128)(2,1)S(1)}, bf16[4,512,128]{2,1,0:T(8,128)(2,1)S(1)}, u32[]{:S(2)}, u32[]{:S(2)}) collective-permute-start(bf16[4,512,128]{2,1,0:T(8,128)(2,1)S(1)} %collective-permute-done), channel_id=1, source_target_pairs={{112,0},{113,1},{114,2},{115,3},{116,4},{117,5},{118,6},{119,7},{1... | collective-permute-start | bytes 1572872 | tf_op jit(solution)/shard_map/ppermute | solution.py:27
  74.5 14.2 %collective-permute-start.3 = (bf16[4,512,128]{2,1,0:T(8,128)(2,1)S(1)}, bf16[4,512,128]{2,1,0:T(8,128)(2,1)S(1)}, u32[]{:S(2)}, u32[]{:S(2)}) collective-permute-start(bf16[4,512,128]{2,1,0:T(8,128)(2,1)S(1)} %collective-permute-done.1), channel_id=1, source_target_pairs={{16,0},{17,1},{18,2},{19,3},{20,4},{21,5},{22,6},{23,7},{24,8},{25... | collective-permute-start | bytes 1572872 | tf_op jit(solution)/shard_map/ppermute | solution.py:27
  88.4 13.4 %collective-permute-start.4 = (bf16[4,512,128]{2,1,0:T(8,128)(2,1)S(1)}, bf16[4,512,128]{2,1,0:T(8,128)(2,1)S(1)}, u32[]{:S(2)}, u32[]{:S(2)}) collective-permute-start(bf16[4,512,128]{2,1,0:T(8,128)(2,1)S(1)} %collective-permute-done.2), channel_id=1, source_target_pairs={{112,0},{113,1},{114,2},{115,3},{116,4},{117,5},{118,6},{119,7},{1... | collective-permute-start | bytes 1572872 | tf_op jit(solution)/shard_map/ppermute | solution.py:27
  88.8 13.7 %collective-permute-start.5 = (bf16[4,512,128]{2,1,0:T(8,128)(2,1)S(1)}, bf16[4,512,128]{2,1,0:T(8,128)(2,1)S(1)}, u32[]{:S(2)}, u32[]{:S(2)}) collective-permute-start(bf16[4,512,128]{2,1,0:T(8,128)(2,1)S(1)} %collective-permute-done.3), channel_id=1, source_target_pairs={{16,0},{17,1},{18,2},{19,3},{20,4},{21,5},{22,6},{23,7},{24,8},{25... | collective-permute-start | bytes 1572872 | tf_op jit(solution)/shard_map/ppermute | solution.py:27
  101.8 12.5 %collective-permute-start.6 = (bf16[4,512,128]{2,1,0:T(8,128)(2,1)S(1)}, bf16[4,512,128]{2,1,0:T(8,128)(2,1)S(1)}, u32[]{:S(2)}, u32[]{:S(2)}) collective-permute-start(bf16[4,512,128]{2,1,0:T(8,128)(2,1)S(1)} %collective-permute-done.4), channel_id=1, source_target_pairs={{112,0},{113,1},{114,2},{115,3},{116,4},{117,5},{118,6},{119,7},{1... | collective-permute-start | bytes 1572872 | tf_op jit(solution)/shard_map/ppermute | solution.py:27
where the time goes:
time: 147 us; the launch traced here: 146 us
  waiting for transfers between devices  65.1 us (44%)
  starting transfers between devices  34.8 us (24%)
  blocking collectives  22.1 us (15%)
  matrix products  12 us (8%)
  local copies, waits for them, and re-layouts  10.1 us (7%)
  other arithmetic  1.74 us (1%)
    ppermute x7, waiting for transfers between devices, shifted(): return lax.ppermute(block, axis, route)  44.5 us
    all_to_all x1, starting transfers between devices, in_one_piece(): lax.all_to_all(both, axis, split_axis=split_dim, concat_axis=concat_dim,...  27.4 us
    all_to_all x1, blocking collectives, shards(): lax.all_to_all(attended.reshape(devices, sub_rows, 1, head_size), 'seq',...  22.1 us
    all_to_all x1, waiting for transfers between devices, in_one_piece(): lax.all_to_all(both, axis, split_axis=split_dim, concat_axis=concat_dim,...  20.6 us
    ppermute x7, starting transfers between devices, shifted(): return lax.ppermute(block, axis, route)  7.33 us
    unnamed x14, local copies, waits for them, and re-layouts  6.24 us
    dot_general x8, matrix products, absorb(): jnp.dot(jnp.where(is_fresh, rounded, zeroes), key_block[1], preferred_ele...  3.63 us
    dot_general x8, matrix products, absorb(): jnp.dot(jnp.where(is_fresh, zeroes, rounded), key_block[3], preferred_ele...  3.52 us
  transfers between devices with their start and end apart: 8, of which 5 were waited for; matrix products, arithmetic and copies ran while one was open for 4% of the time, Pallas kernels for 0%

commit v1 on v0

v1 whole, which is shorter than its diff:
```python
import functools
import math

import jax
import jax.numpy as jnp
from jax import lax
from jax.experimental import pallas as pl
from jax.experimental.pallas import tpu as pltpu
from jax.sharding import PartitionSpec as P

HEAD = 128
SUBS = 4
MESH = pl.DeviceIdType.MESH


def kernel(
    side,
    local,
    sizes,
    q_in,
    fk_in,
    fv_in,
    sk_in,
    sv_in,
    out,
    stage,
    qall,
    kv,
    vaug,
    opart,
    lpart,
    orecv,
    lrecv,
    outst,
    load_sem,
    self_sem,
    p1_send,
    p1_recv,
    ring_send,
    ring_recv,
    part_send,
    part_recv,
    p4_send,
    p4_recv,
):
    group = lax.axis_index("groups")
    me = lax.axis_index("seq")
    c = me % 2
    x = (me // 2) % side
    y = me // 2 // side
    a = x * (1 - c) + y * c
    g = y * (1 - c) + x * c
    rows = 2 * side * local
    half = side // 2
    pair = 2 * local
    scale2 = (HEAD**-0.5) * math.log2(math.e)

    def at(cx, cy, core):
        return (group, (cy * side + cx) * 2 + core)

    def line(a_to, g_to, core):
        return at(a_to * (1 - c) + g_to * c, g_to * (1 - c) + a_to * c, core)

    def head_cols(head):
        return pl.ds(pl.multiple_of(head * HEAD, HEAD), HEAD)

    loads = []
    for i, ref in enumerate((q_in, fk_in, fv_in, sk_in, sv_in)):
        loads.append(pltpu.make_async_copy(ref, stage.at[i], load_sem.at[i]))
        loads[-1].start()

    barrier = pltpu.get_barrier_semaphore()
    for j in range(1, side):
        for core in range(2):
            pl.semaphore_signal(barrier, inc=1, device_id=at((x + j) % side, y, core), device_id_type=MESH)
            pl.semaphore_signal(barrier, inc=1, device_id=at(x, (y + j) % side, core), device_id_type=MESH)
    pl.semaphore_signal(barrier, inc=1, device_id=at(x, y, 1 - c), device_id_type=MESH)

    own_row = pl.ds(pl.multiple_of((a * 2 + c) * local, local), local)
    own_head = c * side + a
    own = []
    for i, ref in enumerate((q_in, fk_in, fv_in, sk_in, sv_in)):
        dst = qall.at[g, own_row, :] if i == 0 else kv.at[i - 1, own_row, :]
        own.append(pltpu.make_async_copy(ref.at[:, head_cols(own_head)], dst, self_sem.at[i]))
        own[-1].start()
    vaug[:, HEAD:] = jnp.ones((2 * rows, HEAD), jnp.bfloat16)

    for copy in loads:
        copy.wait()
    pl.semaphore_wait(barrier, 4 * (side - 1) + 1)

    row_x = pl.ds(pl.multiple_of((x * 2 + c) * local, local), local)
    row_y = pl.ds(pl.multiple_of((y * 2 + c) * local, local), local)

    order = []
    for j in range(1, half + 1):
        order.append(j)
        if j != side - j:
            order.append(side - j)

    def send_slices(which):
        def go(device, head, slot, row):
            if which == 0:
                src, dst = stage.at[0, :, head_cols(head)], qall.at[slot, row, :]
            else:
                src, dst = stage.at[pl.ds(1, 4), :, head_cols(head)], kv.at[:, row, :]
            pltpu.make_async_remote_copy(
                src_ref=src,
                dst_ref=dst,
                send_sem=p1_send.at[which],
                recv_sem=p1_recv.at[which],
                device_id=device,
                device_id_type=MESH,
            ).start()

        for j in order:
            to_x, to_y = (x + j) % side, (y + j) % side
            go(at(to_x, y, 0), to_x, y, row_x)
            go(at(x, to_y, 1), side + to_y, x, row_y)
        d = 1 - c
        go(
            at(x, y, d),
            d * side + x * (1 - d) + y * d,
            y * (1 - d) + x * d,
            pl.ds(pl.multiple_of(((x * (1 - d) + y * d) * 2 + c) * local, local), local),
        )

    send_slices(0)
    send_slices(1)

    sub_rows = rows // SUBS

    def subs_of(direction, step):
        if step < half:
            return list(range(SUBS))
        return list(range(SUBS // 2)) if direction == 0 else list(range(SUBS // 2, SUBS))

    def sub_ref(chunk, sub):
        return qall.at[chunk, pl.ds(sub * sub_rows, sub_rows), :]

    def ring(direction, step, sub):
        if direction == 0:
            chunk, to = (g + side - (step - 1)) % side, (g + 1) % side
        else:
            chunk, to = (g + step - 1) % side, (g + side - 1) % side
        return pltpu.make_async_remote_copy(
            src_ref=sub_ref(chunk, sub),
            dst_ref=sub_ref(chunk, sub),
            send_sem=ring_send.at[direction, step - 1, sub],
            recv_sem=ring_recv.at[direction, step - 1, sub],
            device_id=line(a, to, c),
            device_id_type=MESH,
        )

    def ring_wait(direction, step, sub):
        chunk = (g + side - step) % side if direction == 0 else (g + step) % side
        ref = sub_ref(chunk, sub)
        pltpu.make_async_copy(ref, ref, ring_recv.at[direction, step - 1, sub]).wait()

    sent = []

    def ring_start(step):
        for sub in range(SUBS):
            for direction in range(2):
                if step > 1 and step - 1 < half:
                    ring_wait(direction, step - 1, sub)
                if step <= half and sub in subs_of(direction, step):
                    copy = ring(direction, step, sub)
                    copy.start()
                    sent.append(copy)

    own[0].wait()
    others = rows - local
    ref = qall.at[0, pl.ds(0, others), :]
    pltpu.make_async_copy(ref, ref, p1_recv.at[0]).wait()
    ring_start(1)
    ring_start(2)

    for copy in own[1:]:
        copy.wait()
    ref = kv.at[:, pl.ds(0, others), :]
    pltpu.make_async_copy(ref, ref, p1_recv.at[1]).wait()
    vaug[pl.ds(0, rows), pl.ds(0, HEAD)] = kv[1]
    vaug[pl.ds(rows, rows), pl.ds(0, HEAD)] = kv[3]

    step_a = pair * (1 + c * (side - 1))
    step_g = pair * (side - c * (side - 1))
    end0 = sizes[0]
    end1 = end0 + sizes[1]
    end2 = end1 + sizes[2]
    big = jnp.int32(2**30)

    def position(l, chunk):
        return (l // pair) * step_a + chunk * step_g + l % pair

    key_pos = position(lax.broadcasted_iota(jnp.int32, (8, rows), 1), g)[0:1, :]
    eye = lax.broadcasted_iota(jnp.int32, (HEAD, HEAD), 0) == lax.broadcasted_iota(jnp.int32, (HEAD, HEAD), 1)
    contract = (((1,), (1,)), ((), ()))
    qt = min(256, rows)

    def compute(chunk, o_ref, l_ref):
        def tile(t, _):
            start = pl.multiple_of(t * qt, qt)
            q = qall[chunk, pl.ds(start, qt), :]
            pos = position(lax.broadcasted_iota(jnp.int32, (qt, HEAD), 0) + start, chunk)
            thr = jnp.where(pos < end0, end0, jnp.where(pos < end1, end1, jnp.where(pos < end2, end2, big)))
            thr = jnp.concatenate([thr] * (rows // HEAD), axis=1)
            fresh = key_pos < thr
            sf = lax.dot_general(q, kv[0], contract, preferred_element_type=jnp.float32)
            ss = lax.dot_general(q, kv[2], contract, preferred_element_type=jnp.float32)
            s = jnp.where(fresh, sf, ss)
            m = jnp.max(s, axis=1, keepdims=True)
            p = jnp.exp2((s - m) * scale2)
            pf = jnp.where(fresh, p, 0.0)
            both = jnp.concatenate([pf.astype(jnp.bfloat16), (p - pf).astype(jnp.bfloat16)], axis=1)
            o = jnp.dot(both, vaug[...], preferred_element_type=jnp.float32)
            total = o[:, HEAD:]
            o_ref[pl.ds(start, qt), :] = (o[:, :HEAD] / total).astype(jnp.bfloat16)
            lse = m * scale2 + jnp.log2(total)
            for k in range(qt // HEAD):
                block = lse[k * HEAD : (k + 1) * HEAD, :]
                l_ref[pl.ds(t * (qt // HEAD) + k, 1), :] = jnp.sum(jnp.where(eye, block, 0.0), axis=0, keepdims=True)
            return 0

        lax.fori_loop(0, rows // qt, tile, 0)

    def part_copies(delta):
        to = line(a, (g + side - delta) % side, c)
        kinds = ((opart, orecv), (lpart, lrecv))
        return [
            pltpu.make_async_remote_copy(
                src_ref=src.at[delta],
                dst_ref=dst.at[delta],
                send_sem=part_send.at[kind, delta],
                recv_sem=part_recv.at[kind, delta],
                device_id=to,
                device_id_type=MESH,
            )
            for kind, (src, dst) in enumerate(kinds)
        ]

    def do_part(delta):
        compute((g + side - delta) % side, opart.at[delta], lpart.at[delta])
        for copy in part_copies(delta):
            copy.start()
            sent.append(copy)

    compute(g, orecv.at[0], lrecv.at[0])
    for step in range(1, half):
        ring_start(step + 2)
        do_part(step)
        do_part(side - step)
    for direction in range(2):
        for sub in subs_of(direction, half):
            ring_wait(direction, half, sub)
    do_part(half)

    for delta in range(1, side):
        for kind, ref in enumerate((orecv, lrecv)):
            pltpu.make_async_copy(ref.at[delta], ref.at[delta], part_recv.at[kind, delta]).wait()
    lse = [lrecv[delta] for delta in range(side)]
    top = functools.reduce(jnp.maximum, lse)
    weights = [jnp.exp2(l - top) for l in lse]
    total = functools.reduce(jnp.add, weights)
    weights = [w / total for w in weights]
    for t in range(rows // HEAD):
        acc = jnp.zeros((HEAD, HEAD), jnp.float32)
        for delta in range(side):
            w = jnp.sum(jnp.where(eye, weights[delta][t : t + 1, :], 0.0), axis=1, keepdims=True)
            acc = acc + w * orecv[delta, pl.ds(t * HEAD, HEAD), :].astype(jnp.float32)
        outst[pl.ds(t * HEAD, HEAD), :] = acc.astype(jnp.bfloat16)

    def home(a_to, core):
        row = pl.ds(pl.multiple_of((a_to * 2 + core) * local, local), local)
        pltpu.make_async_remote_copy(
            src_ref=outst.at[row, :],
            dst_ref=out.at[:, head_cols(own_head)],
            send_sem=p4_send,
            recv_sem=p4_recv,
            device_id=line(a_to, g, core),
            device_id_type=MESH,
        ).start()

    for j in order:
        for core in range(2):
            home((a + j) % side, core)
    home(a, 1 - c)
    out[:, head_cols(own_head)] = outst[own_row, :]

    ref = qall.at[0, pl.ds(0, others), :]
    pltpu.make_async_copy(ref, ref, p1_send.at[0]).wait()
    ref = kv.at[:, pl.ds(0, others), :]
    pltpu.make_async_copy(ref, ref, p1_send.at[1]).wait()
    for copy in sent:
        copy.wait_send()
    ref = outst.at[pl.ds(0, others), :]
    pltpu.make_async_copy(ref, ref, p4_recv).wait()
    pltpu.make_async_copy(ref, ref, p4_send).wait()


def shards(queries, fresh_keys, fresh_values, stale_keys, stale_values, patch_sizes):
    local, columns = queries.shape
    chips = lax.axis_size("seq") // 2
    side = math.isqrt(chips)
    assert side * side == chips and columns == 2 * side * HEAD
    rows = 2 * side * local
    half = side // 2
    bf16, f32 = jnp.bfloat16, jnp.float32
    dma = pltpu.SemaphoreType.DMA
    return pl.pallas_call(
        functools.partial(kernel, side, local),
        out_shape=jax.ShapeDtypeStruct((local, columns), bf16),
        in_specs=[pl.BlockSpec(memory_space=pltpu.SMEM)] + [pl.BlockSpec(memory_space=pl.ANY)] * 5,
        out_specs=pl.BlockSpec(memory_space=pltpu.VMEM),
        scratch_shapes=[
            pltpu.VMEM((5, local, columns), bf16),
            pltpu.VMEM((side, rows, HEAD), bf16),
            pltpu.VMEM((4, rows, HEAD), bf16),
            pltpu.VMEM((2 * rows, 2 * HEAD), bf16),
            pltpu.VMEM((side, rows, HEAD), bf16),
            pltpu.VMEM((side, rows // HEAD, HEAD), f32),
            pltpu.VMEM((side, rows, HEAD), bf16),
            pltpu.VMEM((side, rows // HEAD, HEAD), f32),
            pltpu.VMEM((rows, HEAD), bf16),
            dma((5,)),
            dma((5,)),
            dma((2,)),
            dma((2,)),
            dma((2, half, SUBS)),
            dma((2, half, SUBS)),
            dma((2, side)),
            dma((2, side)),
            dma,
            dma,
        ],
        compiler_params=pltpu.CompilerParams(collective_id=0, has_side_effects=True),
    )(patch_sizes, queries, fresh_keys, fresh_values, stale_keys, stale_values)


def solution(mesh):
    in_specs = (
        P(("groups", "seq"), None),
        P(("groups", "seq"), None),
        P(("groups", "seq"), None),
        P(("groups", "seq"), None),
        P(("groups", "seq"), None),
        P("groups"),
    )
    out_specs = P(("groups", "seq"), None)
    return jax.shard_map(shards, mesh=mesh, in_specs=in_specs, out_specs=out_specs, check_vma=False)
```

time: 147 us -> 66.7 us (0.45)
  waiting for transfers between devices: 65.1 us -> 0 us
  Pallas kernels: 0 us -> 65 us
  starting transfers between devices: 34.8 us -> 0 us
  blocking collectives: 22.1 us -> 0 us
  matrix products: 12 us -> 0 us
  local copies, waits for them, and re-layouts: 10.1 us -> 1.57 us
  other arithmetic: 1.74 us -> 0 us
    pallas_call x0 -> x1, Pallas kernels: none -> 65 us  [shards(): pl.pallas_call(functools.partial(kernel, side, local), out_shape=jax.Shap...]
    ppermute x7 -> x0, waiting for transfers between devices: 44.5 us -> none  [shifted(): return lax.ppermute(block, axis, route)]
    all_to_all x1 -> x0, starting transfers between devices: 27.4 us -> none  [in_one_piece(): lax.all_to_all(both, axis, split_axis=split_dim, concat_axis=concat_dim,...]
    all_to_all x1 -> x0, blocking collectives: 22.1 us -> none  [shards(): lax.all_to_all(attended.reshape(devices, sub_rows, 1, head_size), 'seq',...]
    all_to_all x1 -> x0, waiting for transfers between devices: 20.6 us -> none  [in_one_piece(): lax.all_to_all(both, axis, split_axis=split_dim, concat_axis=concat_dim,...]
    dot_general x32 -> x0, matrix products: 12 us -> none  [the longest x8 3.63 us: absorb(): jnp.dot(jnp.where(is_fresh, rounded, zeroes), key_block[1], preferred_ele...]
    ppermute x7 -> x0, starting transfers between devices: 7.33 us -> none  [shifted(): return lax.ppermute(block, axis, route)]
    unnamed x14 -> x1, local copies, waits for them, and re-layouts: 6.24 us -> 1.57 us
  transfers between devices with their start and end apart: 8 -> 0, of which waited for: 5 -> 0; matrix products, arithmetic and copies ran while one was open for 4% -> 0% of each run, Pallas kernels for 0% -> 0%
where the time goes in v1:
time: 66.7 us; the launch traced here: 66.6 us
  Pallas kernels  65 us (97%)
  local copies, waits for them, and re-layouts  1.57 us (2%)
    pallas_call x1, Pallas kernels, shards(): pl.pallas_call(functools.partial(kernel, side, local), out_shape=jax.Shap...  65 us
    unnamed x1, local copies, waits for them, and re-layouts  1.57 us

profile of v1, /device:TPU:513, one launch (start us, length us, event | category | flops | bytes accessed | tf_op | source)
XLA Modules:
  0.0 66.6 jit_solution(2276650823234604896)
XLA Ops:
  0.0 65.0 %shard_map.64 = bf16[32,2048]{1,0:T(8,128)(2,1)} custom-call(s32[4]{0:T(128)} %sizes.1, bf16[32,2048]{1,0:T(8,128)(2,1)} %q_in.1, bf16[32,2048]{1,0:T(8,128)(2,1)} %fk_in.1, bf16[32,2048]{1,0:T(8,128)(2,1)} %fv_in.1, bf16[32,2048]{1,0:T(8,128)(2,1)} %sk_in.1, bf16[32,2048]{1,0:T(8,128)(2,1)} %sv_in.1), custom_call_target="tpu_custom_call" | custom-call | tf_op jit(solution)/shard_map/pallas_call | solution.py:310
  65.0 1.6 %copy.8 = bf16[32,2048]{1,0:T(8,128)(2,1)} copy(bf16[32,2048]{1,0:T(8,128)(2,1)} %shard_map.64) | data formatting | bytes 262144

commit v2 on v1

--- a/solution.py
+++ b/solution.py
@@ -10,6 +10,8 @@
 
 HEAD = 128
 SUBS = 4
+PATCHES = 4
+QT = 512
 MESH = pl.DeviceIdType.MESH
 
 
@@ -26,7 +28,8 @@
     stage,
     qall,
     kv,
-    vaug,
+    kcat,
+    vcat,
     opart,
     lpart,
     orecv,
@@ -83,7 +86,6 @@
         dst = qall.at[g, own_row, :] if i == 0 else kv.at[i - 1, own_row, :]
         own.append(pltpu.make_async_copy(ref.at[:, head_cols(own_head)], dst, self_sem.at[i]))
         own[-1].start()
-    vaug[:, HEAD:] = jnp.ones((2 * rows, HEAD), jnp.bfloat16)
 
     for copy in loads:
         copy.wait()
@@ -180,49 +182,58 @@
         copy.wait()
     ref = kv.at[:, pl.ds(0, others), :]
     pltpu.make_async_copy(ref, ref, p1_recv.at[1]).wait()
-    vaug[pl.ds(0, rows), pl.ds(0, HEAD)] = kv[1]
-    vaug[pl.ds(rows, rows), pl.ds(0, HEAD)] = kv[3]
 
     step_a = pair * (1 + c * (side - 1))
     step_g = pair * (side - c * (side - 1))
     end0 = sizes[0]
     end1 = end0 + sizes[1]
     end2 = end1 + sizes[2]
-    big = jnp.int32(2**30)
-
-    def position(l, chunk):
-        return (l // pair) * step_a + chunk * step_g + l % pair
-
-    key_pos = position(lax.broadcasted_iota(jnp.int32, (8, rows), 1), g)[0:1, :]
+
+    def patches(count, start, chunk):
+        l = lax.broadcasted_iota(jnp.int32, (count, HEAD), 0) + start
+        pos = (l // pair) * step_a + chunk * step_g + l % pair
+        one, zero = jnp.int32(1), jnp.int32(0)
+        return sum(jnp.where(pos >= end, one, zero) for end in (end0, end1, end2))
+
+    def indicator(mask):
+        return jnp.where(mask, 1.0, 0.0).astype(jnp.bfloat16)
+
+    key_patch = patches(rows, 0, g)
+    for p in range(PATCHES):
+        cols = pl.ds(p * HEAD, HEAD)
+        fresh, stale = indicator(key_patch <= p), indicator(key_patch > p)
+        kcat[:, cols] = kv[0] * fresh + kv[2] * stale
+        vcat[:, cols] = kv[1] * fresh + kv[3] * stale
+
     eye = lax.broadcasted_iota(jnp.int32, (HEAD, HEAD), 0) == lax.broadcasted_iota(jnp.int32, (HEAD, HEAD), 1)
     contract = (((1,), (1,)), ((), ()))
-    qt = min(256, rows)
+    qt = min(QT, rows)
 
     def compute(chunk, o_ref, l_ref):
         def tile(t, _):
-            start = pl.multiple_of(t * qt, qt)
+            start = t * qt if isinstance(t, int) else pl.multiple_of(t * qt, qt)
             q = qall[chunk, pl.ds(start, qt), :]
-            pos = position(lax.broadcasted_iota(jnp.int32, (qt, HEAD), 0) + start, chunk)
-            thr = jnp.where(pos < end0, end0, jnp.where(pos < end1, end1, jnp.where(pos < end2, end2, big)))
-            thr = jnp.concatenate([thr] * (rows // HEAD), axis=1)
-            fresh = key_pos < thr
-            sf = lax.dot_general(q, kv[0], contract, preferred_element_type=jnp.float32)
-            ss = lax.dot_general(q, kv[2], contract, preferred_element_type=jnp.float32)
-            s = jnp.where(fresh, sf, ss)
+            patch = patches(qt, start, chunk)
+            split = jnp.concatenate([q * indicator(patch == p) for p in range(PATCHES)], axis=1)
+            s = lax.dot_general(split, kcat[...], contract, preferred_element_type=jnp.float32)
             m = jnp.max(s, axis=1, keepdims=True)
-            p = jnp.exp2((s - m) * scale2)
-            pf = jnp.where(fresh, p, 0.0)
-            both = jnp.concatenate([pf.astype(jnp.bfloat16), (p - pf).astype(jnp.bfloat16)], axis=1)
-            o = jnp.dot(both, vaug[...], preferred_element_type=jnp.float32)
-            total = o[:, HEAD:]
-            o_ref[pl.ds(start, qt), :] = (o[:, :HEAD] / total).astype(jnp.bfloat16)
+            w = jnp.exp2((s - m) * scale2)
+            total = jnp.sum(w, axis=1, keepdims=True)
+            o = jnp.dot(w.astype(jnp.bfloat16), vcat[...], preferred_element_type=jnp.float32)
+            picked = o[:, :HEAD]
+            for p in range(1, PATCHES):
+                picked = jnp.where(patch == p, o[:, p * HEAD : (p + 1) * HEAD], picked)
+            o_ref[pl.ds(start, qt), :] = (picked / total).astype(jnp.bfloat16)
             lse = m * scale2 + jnp.log2(total)
             for k in range(qt // HEAD):
                 block = lse[k * HEAD : (k + 1) * HEAD, :]
                 l_ref[pl.ds(t * (qt // HEAD) + k, 1), :] = jnp.sum(jnp.where(eye, block, 0.0), axis=0, keepdims=True)
             return 0
 
-        lax.fori_loop(0, rows // qt, tile, 0)
+        if rows == qt:
+            tile(0, 0)
+        else:
+            lax.fori_loop(0, rows // qt, tile, 0)
 
     def part_copies(delta):
         to = line(a, (g + side - delta) % side, c)
@@ -316,7 +327,8 @@
             pltpu.VMEM((5, local, columns), bf16),
             pltpu.VMEM((side, rows, HEAD), bf16),
             pltpu.VMEM((4, rows, HEAD), bf16),
-            pltpu.VMEM((2 * rows, 2 * HEAD), bf16),
+            pltpu.VMEM((rows, PATCHES * HEAD), bf16),
+            pltpu.VMEM((rows, PATCHES * HEAD), bf16),
             pltpu.VMEM((side, rows, HEAD), bf16),
             pltpu.VMEM((side, rows // HEAD, HEAD), f32),
             pltpu.VMEM((side, rows, HEAD), bf16),

time: 66.7 us -> 64.7 us (0.970)
  Pallas kernels: 65 us -> 63 us
    pallas_call x1, Pallas kernels: 65 us -> 63 us  [shards(): pl.pallas_call(functools.partial(kernel, side, local), out_shape=jax.Shap...]
where the time goes in v2:
time: 64.7 us; the launch traced here: 64.6 us
  Pallas kernels  63 us (97%)
  local copies, waits for them, and re-layouts  1.57 us (2%)
    pallas_call x1, Pallas kernels, shards(): pl.pallas_call(functools.partial(kernel, side, local), out_shape=jax.Shap...  63 us
    unnamed x1, local copies, waits for them, and re-layouts  1.57 us

profile of v2, /device:TPU:513, one launch (start us, length us, event | category | flops | bytes accessed | tf_op | source)
XLA Modules:
  0.0 64.6 jit_solution(15317746164224585505)
XLA Ops:
  0.0 63.0 %shard_map.64 = bf16[32,2048]{1,0:T(8,128)(2,1)} custom-call(s32[4]{0:T(128)} %sizes.1, bf16[32,2048]{1,0:T(8,128)(2,1)} %q_in.1, bf16[32,2048]{1,0:T(8,128)(2,1)} %fk_in.1, bf16[32,2048]{1,0:T(8,128)(2,1)} %fv_in.1, bf16[32,2048]{1,0:T(8,128)(2,1)} %sk_in.1, bf16[32,2048]{1,0:T(8,128)(2,1)} %sv_in.1), custom_call_target="tpu_custom_call" | custom-call | tf_op jit(solution)/shard_map/pallas_call | solution.py:321
  63.0 1.6 %copy.8 = bf16[32,2048]{1,0:T(8,128)(2,1)} copy(bf16[32,2048]{1,0:T(8,128)(2,1)} %shard_map.64) | data formatting | bytes 262144

commit v3 on v2

v3 whole, which is shorter than its diff:
```python
import functools
import math

import jax
import jax.numpy as jnp
from jax import lax
from jax.experimental import pallas as pl
from jax.experimental.pallas import tpu as pltpu
from jax.sharding import PartitionSpec as P

HEAD = 128
SUBS = 4
PATCHES = 4
MESH = pl.DeviceIdType.MESH


def kernel(
    side,
    local,
    sizes,
    q_in,
    fk_in,
    fv_in,
    sk_in,
    sv_in,
    out,
    stage,
    qall,
    kv,
    kcat,
    vcat,
    opart,
    lpart,
    orecv,
    lrecv,
    outst,
    load_sem,
    self_sem,
    p1_send,
    p1_recv,
    ready,
    ring_send,
    ring_recv,
    direct_send,
    direct_recv,
    part_send,
    part_recv,
    p4_send,
    p4_recv,
):
    group = lax.axis_index("groups")
    me = lax.axis_index("seq")
    c = me % 2
    x = (me // 2) % side
    y = me // 2 // side
    a = x * (1 - c) + y * c
    g = y * (1 - c) + x * c
    rows = 2 * side * local
    pair = 2 * local
    scale2 = (HEAD**-0.5) * math.log2(math.e)

    def at(cx, cy, core):
        return (group, (cy * side + cx) * 2 + core)

    def line(a_to, g_to, core):
        return at(a_to * (1 - c) + g_to * c, g_to * (1 - c) + a_to * c, core)

    def head_cols(head):
        return pl.ds(pl.multiple_of(head * HEAD, HEAD), HEAD)

    inputs = (q_in, fk_in, fv_in, sk_in, sv_in)
    loads = [pltpu.make_async_copy(ref, stage.at[i], load_sem.at[i]) for i, ref in enumerate(inputs)]
    for copy in loads:
        copy.start()

    def block(index):
        return pl.ds(pl.multiple_of(index * local, local), local)

    def signal(semaphore, device):
        pl.semaphore_signal(semaphore, inc=1, device_id=device, device_id_type=MESH)

    def loop(first, last, body):
        def step(i, carry):
            body(i)
            return carry

        lax.fori_loop(first, last, step, 0)

    barrier = pltpu.get_barrier_semaphore()

    def greet_row(i):
        signal(barrier, at(i, y, 0))
        signal(barrier, at(i, y, 1))

    def greet_column(i):
        signal(barrier, at(x, i, 0))
        signal(barrier, at(x, i, 1))

    loop(0, x, greet_row)
    loop(0, y, greet_column)

    @pl.when(c == 1)
    def _():
        signal(barrier, at(x, y, 0))

    own_row = block(a * 2 + c)
    own_head = c * side + a
    own = []
    for i, ref in enumerate(inputs):
        dst = qall.at[g, own_row, :] if i == 0 else kv.at[i - 1, own_row, :]
        own.append(pltpu.make_async_copy(ref.at[:, head_cols(own_head)], dst, self_sem.at[i]))
        own[-1].start()

    higher = 2 * (side - 1 - x) + 2 * (side - 1 - y) + (1 - c)

    @pl.when(higher > 0)
    def _():
        pl.semaphore_wait(barrier, higher)

    def ready_row(i):
        signal(ready.at[x * 2 + c], at(i, y, 0))
        signal(ready.at[x * 2 + c], at(i, y, 1))

    def ready_column(i):
        signal(ready.at[2 * side + y * 2 + c], at(x, i, 0))
        signal(ready.at[2 * side + y * 2 + c], at(x, i, 1))

    loop(x + 1, side, ready_row)
    loop(y + 1, side, ready_column)

    @pl.when(c == 0)
    def _():
        signal(ready.at[x * 2], at(x, y, 1))

    row_x, row_y = block(x * 2 + c), block(y * 2 + c)

    def push(which, device, head, slot, row):
        if which == 0:
            src, dst = stage.at[0, :, head_cols(head)], qall.at[slot, row, :]
        else:
            src, dst = stage.at[pl.ds(1, 4), :, head_cols(head)], kv.at[:, row, :]
        pltpu.make_async_remote_copy(
            src_ref=src,
            dst_ref=dst,
            send_sem=p1_send.at[which],
            recv_sem=p1_recv.at[which],
            device_id=device,
            device_id_type=MESH,
        ).start()

    def push_row(which, i):
        push(which, at(i, y, 0), i, y, row_x)

    def push_column(which, i):
        push(which, at(x, i, 1), side + i, x, row_y)

    for which in range(2):
        for copy in loads[:1] if which == 0 else loads[1:]:
            copy.wait()
        loop(x + 1, side, functools.partial(push_row, which))
        loop(y + 1, side, functools.partial(push_column, which))

        @pl.when(c == 0)
        def _():
            push_column(which, y)

    def hear(index):
        pl.semaphore_wait(ready.at[index], 1)

    def lower_row(k):
        i = x - 1 - k

        @pl.when(i + y > 0)
        def _():
            hear(i * 2)
            hear(i * 2 + 1)
            push_row(0, i)
            push_row(1, i)

    def lower_column(k):
        i = y - 1 - k

        @pl.when(i + x > 0)
        def _():
            hear(2 * side + i * 2)

        hear(2 * side + i * 2 + 1)
        push_column(0, i)
        push_column(1, i)

    loop(0, x, lower_row)
    loop(0, y, lower_column)

    @pl.when((c == 1) & (me > 1))
    def _():
        hear(x * 2)
        push_row(0, x)
        push_row(1, x)

    members = side - 1
    steps = (members - 1) // 2
    sub_rows = rows // SUBS
    others = rows - local

    def sub_ref(chunk, sub):
        return qall.at[chunk, pl.ds(sub * sub_rows, sub_rows), :]

    def member(offset):
        return (g - 1 + 2 * members + offset) % members + 1

    def ring(direction, step, sub):
        sign = 1 - 2 * direction
        ref = sub_ref(member(-sign * (step - 1)), sub)
        return pltpu.make_async_remote_copy(
            src_ref=ref,
            dst_ref=ref,
            send_sem=ring_send.at[direction, step - 1, sub],
            recv_sem=ring_recv.at[direction, step - 1, sub],
            device_id=line(a, member(sign), c),
            device_id_type=MESH,
        )

    def ring_wait(direction, step, sub):
        ref = sub_ref(member((2 * direction - 1) * step), sub)
        pltpu.make_async_copy(ref, ref, ring_recv.at[direction, step - 1, sub]).wait()

    def wait_own_queries():
        own[0].wait()
        ref = qall.at[0, pl.ds(0, others), :]
        pltpu.make_async_copy(ref, ref, p1_recv.at[0]).wait()

    @pl.when(g > 0)
    def _():
        wait_own_queries()
        for step in range(1, steps + 2):
            for sub in range(SUBS):
                for direction in range(2):
                    if step > 1:
                        ring_wait(direction, step - 1, sub)
                    if step <= steps:
                        ring(direction, step, sub).start()

    @pl.when((y == 0) & (me > 0))
    def _():
        hear(0)

        @pl.when(x > 0)
        def _():
            hear(1)

        push_row(0, 0)
        push_row(1, 0)

    @pl.when((x == 0) & (y > 0))
    def _():
        hear(2 * side)

    def direct(chunk, to):
        return pltpu.make_async_remote_copy(
            src_ref=qall.at[chunk],
            dst_ref=qall.at[chunk],
            send_sem=direct_send.at[to],
            recv_sem=direct_recv.at[chunk],
            device_id=line(a, to, c),
            device_id_type=MESH,
        )

    @pl.when(g > 0)
    def _():
        direct(g, 0).start()

    far_first = sorted(range(1, side), key=lambda i: -min(i, side - i))

    @pl.when(g == 0)
    def _():
        wait_own_queries()
        for to in far_first:
            direct(0, to).start()

    for copy in own[1:]:
        copy.wait()
    ref = kv.at[:, pl.ds(0, others), :]
    pltpu.make_async_copy(ref, ref, p1_recv.at[1]).wait()

    step_a = pair * (1 + c * (side - 1))
    step_g = pair * (side - c * (side - 1))
    end0 = sizes[0]
    end1 = end0 + sizes[1]
    end2 = end1 + sizes[2]

    def patches(count, start, chunk):
        l = lax.broadcasted_iota(jnp.int32, (count, HEAD), 0) + start
        pos = (l // pair) * step_a + chunk * step_g + l % pair
        one, zero = jnp.int32(1), jnp.int32(0)
        return sum(jnp.where(pos >= end, one, zero) for end in (end0, end1, end2))

    def indicator(mask):
        return jnp.where(mask, 1.0, 0.0).astype(jnp.bfloat16)

    key_patch = patches(rows, 0, g)
    for p in range(PATCHES):
        cols = pl.ds(p * HEAD, HEAD)
        fresh, stale = indicator(key_patch <= p), indicator(key_patch > p)
        kcat[:, cols] = kv[0] * fresh + kv[2] * stale
        vcat[:, cols] = kv[1] * fresh + kv[3] * stale

    eye = lax.broadcasted_iota(jnp.int32, (HEAD, HEAD), 0) == lax.broadcasted_iota(jnp.int32, (HEAD, HEAD), 1)
    contract = (((1,), (1,)), ((), ()))
    def compute(chunk):
        q = qall[chunk]
        patch = patches(rows, 0, chunk)
        split = jnp.concatenate([q * indicator(patch == p) for p in range(PATCHES)], axis=1)
        s = lax.dot_general(split, kcat[...], contract, preferred_element_type=jnp.float32)
        m = jnp.max(s, axis=1, keepdims=True)
        w = jnp.exp2((s - m) * scale2)
        total = jnp.sum(w, axis=1, keepdims=True)
        o = jnp.dot(w.astype(jnp.bfloat16), vcat[...], preferred_element_type=jnp.float32)
        picked = o[:, :HEAD]
        for p in range(1, PATCHES):
            picked = jnp.where(patch == p, o[:, p * HEAD : (p + 1) * HEAD], picked)
        opart[chunk] = (picked / total).astype(jnp.bfloat16)
        lse = m * scale2 + jnp.log2(total)
        for k in range(rows // HEAD):
            block_lse = lse[k * HEAD : (k + 1) * HEAD, :]
            lpart[chunk, pl.ds(k, 1), :] = jnp.sum(jnp.where(eye, block_lse, 0.0), axis=0, keepdims=True)

    def part(kind, chunk, source):
        src, dst = ((opart, orecv), (lpart, lrecv))[kind]
        return pltpu.make_async_remote_copy(
            src_ref=src.at[chunk],
            dst_ref=dst.at[source],
            send_sem=part_send.at[kind, chunk],
            recv_sem=part_recv.at[kind, source],
            device_id=line(a, chunk, c),
            device_id_type=MESH,
        )

    def one_chunk(k):
        chunk = side - 1 - k

        @pl.when((g == 0) & (chunk > 0))
        def _():
            pltpu.make_async_copy(qall.at[chunk], qall.at[chunk], direct_recv.at[chunk]).wait()

        @pl.when((g > 0) & (chunk == 0))
        def _():
            pltpu.make_async_copy(qall.at[0], qall.at[0], direct_recv.at[0]).wait()

        compute(chunk)

        @pl.when(chunk != g)
        def _():
            part(0, chunk, g).start()
            part(1, chunk, g).start()

    loop(0, side, one_chunk)

    orecv[g] = opart[g]
    lrecv[g] = lpart[g]

    def part_arrived(source):
        @pl.when(source != g)
        def _():
            pltpu.make_async_copy(orecv.at[source], orecv.at[source], part_recv.at[0, source]).wait()
            pltpu.make_async_copy(lrecv.at[source], lrecv.at[source], part_recv.at[1, source]).wait()

    loop(0, side, part_arrived)
    lse = [lrecv[source] for source in range(side)]
    top = functools.reduce(jnp.maximum, lse)
    weights = [jnp.exp2(l - top) for l in lse]
    total = functools.reduce(jnp.add, weights)
    weights = [w / total for w in weights]
    for t in range(rows // HEAD):
        acc = jnp.zeros((HEAD, HEAD), jnp.float32)
        for source in range(side):
            w = jnp.sum(jnp.where(eye, weights[source][t : t + 1, :], 0.0), axis=1, keepdims=True)
            acc = acc + w * orecv[source, pl.ds(t * HEAD, HEAD), :].astype(jnp.float32)
        outst[pl.ds(t * HEAD, HEAD), :] = acc.astype(jnp.bfloat16)

    def home(a_to, core):
        pltpu.make_async_remote_copy(
            src_ref=outst.at[block(a_to * 2 + core), :],
            dst_ref=out.at[:, head_cols(own_head)],
            send_sem=p4_send,
            recv_sem=p4_recv,
            device_id=line(a_to, g, core),
            device_id_type=MESH,
        ).start()

    for j in far_first:
        for core in range(2):
            home((a + j) % side, core)
    home(a, 1 - c)
    out[:, head_cols(own_head)] = outst[own_row, :]

    ref = qall.at[0, pl.ds(0, others), :]
    pltpu.make_async_copy(ref, ref, p1_send.at[0]).wait()
    ref = kv.at[:, pl.ds(0, others), :]
    pltpu.make_async_copy(ref, ref, p1_send.at[1]).wait()

    @pl.when(g > 0)
    def _():
        for step in range(1, steps + 1):
            for sub in range(SUBS):
                for direction in range(2):
                    ring(direction, step, sub).wait_send()
        direct(g, 0).wait_send()

    @pl.when(g == 0)
    def _():
        for to in far_first:
            direct(0, to).wait_send()

    def part_left(chunk):
        @pl.when(chunk != g)
        def _():
            part(0, chunk, g).wait_send()
            part(1, chunk, g).wait_send()

    loop(0, side, part_left)
    ref = outst.at[pl.ds(0, others), :]
    pltpu.make_async_copy(ref, ref, p4_recv).wait()
    pltpu.make_async_copy(ref, ref, p4_send).wait()


def shards(queries, fresh_keys, fresh_values, stale_keys, stale_values, patch_sizes):
    local, columns = queries.shape
    chips = lax.axis_size("seq") // 2
    side = math.isqrt(chips)
    assert side * side == chips and columns == 2 * side * HEAD
    rows = 2 * side * local
    half = side // 2
    bf16, f32 = jnp.bfloat16, jnp.float32
    dma = pltpu.SemaphoreType.DMA
    return pl.pallas_call(
        functools.partial(kernel, side, local),
        out_shape=jax.ShapeDtypeStruct((local, columns), bf16),
        in_specs=[pl.BlockSpec(memory_space=pltpu.SMEM)] + [pl.BlockSpec(memory_space=pl.ANY)] * 5,
        out_specs=pl.BlockSpec(memory_space=pltpu.VMEM),
        scratch_shapes=[
            pltpu.VMEM((5, local, columns), bf16),
            pltpu.VMEM((side, rows, HEAD), bf16),
            pltpu.VMEM((4, rows, HEAD), bf16),
            pltpu.VMEM((rows, PATCHES * HEAD), bf16),
            pltpu.VMEM((rows, PATCHES * HEAD), bf16),
            pltpu.VMEM((side, rows, HEAD), bf16),
            pltpu.VMEM((side, rows // HEAD, HEAD), f32),
            pltpu.VMEM((side, rows, HEAD), bf16),
            pltpu.VMEM((side, rows // HEAD, HEAD), f32),
            pltpu.VMEM((rows, HEAD), bf16),
            dma((5,)),
            dma((5,)),
            dma((2,)),
            dma((2,)),
            pltpu.SemaphoreType.REGULAR((4 * side,)),
            dma((2, half - 1, SUBS)),
            dma((2, half - 1, SUBS)),
            dma((side,)),
            dma((side,)),
            dma((2, side)),
            dma((2, side)),
            dma,
            dma,
        ],
        compiler_params=pltpu.CompilerParams(collective_id=0, has_side_effects=True),
    )(patch_sizes, queries, fresh_keys, fresh_values, stale_keys, stale_values)


def solution(mesh):
    in_specs = (
        P(("groups", "seq"), None),
        P(("groups", "seq"), None),
        P(("groups", "seq"), None),
        P(("groups", "seq"), None),
        P(("groups", "seq"), None),
        P("groups"),
    )
    out_specs = P(("groups", "seq"), None)
    return jax.shard_map(shards, mesh=mesh, in_specs=in_specs, out_specs=out_specs, check_vma=False)
```

time: 64.7 us -> 71.2 us (1.10)
  Pallas kernels: 63 us -> 69.5 us
    pallas_call x1, Pallas kernels: 63 us -> 69.5 us  [shards(): pl.pallas_call(functools.partial(kernel, side, local), out_shape=jax.Shap...]
where the time goes in v3:
time: 71.2 us; the launch traced here: 71 us
  Pallas kernels  69.5 us (98%)
  local copies, waits for them, and re-layouts  1.57 us (2%)
    pallas_call x1, Pallas kernels, shards(): pl.pallas_call(functools.partial(kernel, side, local), out_shape=jax.Shap...  69.5 us
    unnamed x1, local copies, waits for them, and re-layouts  1.57 us

profile of v3, /device:TPU:513, one launch (start us, length us, event | category | flops | bytes accessed | tf_op | source)
XLA Modules:
  0.0 71.0 jit_solution(6328473859737093438)
XLA Ops:
  0.0 69.5 %shard_map.64 = bf16[32,2048]{1,0:T(8,128)(2,1)} custom-call(s32[4]{0:T(128)} %sizes.1, bf16[32,2048]{1,0:T(8,128)(2,1)} %q_in.1, bf16[32,2048]{1,0:T(8,128)(2,1)} %fk_in.1, bf16[32,2048]{1,0:T(8,128)(2,1)} %fv_in.1, bf16[32,2048]{1,0:T(8,128)(2,1)} %sk_in.1, bf16[32,2048]{1,0:T(8,128)(2,1)} %sv_in.1), custom_call_target="tpu_custom_call" | custom-call | tf_op jit(solution)/shard_map/pallas_call | solution.py:435
  69.5 1.6 %copy.8 = bf16[32,2048]{1,0:T(8,128)(2,1)} copy(bf16[32,2048]{1,0:T(8,128)(2,1)} %shard_map.64) | data formatting | bytes 262144

commit v4 on v3

--- a/solution.py
+++ b/solution.py
@@ -41,8 +41,6 @@
     ready,
     ring_send,
     ring_recv,
-    direct_send,
-    direct_recv,
     part_send,
     part_recv,
     p4_send,
@@ -56,6 +54,7 @@
     a = x * (1 - c) + y * c
     g = y * (1 - c) + x * c
     rows = 2 * side * local
+    half = side // 2
     pair = 2 * local
     scale2 = (HEAD**-0.5) * math.log2(math.e)
 
@@ -167,115 +166,65 @@
     def hear(index):
         pl.semaphore_wait(ready.at[index], 1)
 
-    def lower_row(k):
-        i = x - 1 - k
-
-        @pl.when(i + y > 0)
-        def _():
-            hear(i * 2)
-            hear(i * 2 + 1)
-            push_row(0, i)
-            push_row(1, i)
-
-    def lower_column(k):
-        i = y - 1 - k
-
-        @pl.when(i + x > 0)
-        def _():
-            hear(2 * side + i * 2)
-
-        hear(2 * side + i * 2 + 1)
-        push_column(0, i)
-        push_column(1, i)
-
-    loop(0, x, lower_row)
-    loop(0, y, lower_column)
-
-    @pl.when((c == 1) & (me > 1))
+    @pl.when(c == 1)
     def _():
         hear(x * 2)
         push_row(0, x)
         push_row(1, x)
 
-    members = side - 1
-    steps = (members - 1) // 2
-    sub_rows = rows // SUBS
+    def lower_row(k):
+        i = x - 1 - k
+        hear(i * 2 + 1)
+        hear(i * 2)
+        push_row(0, i)
+        push_row(1, i)
+
+    def lower_column(k):
+        i = y - 1 - k
+        hear(2 * side + i * 2 + 1)
+        push_column(0, i)
+        push_column(1, i)
+        hear(2 * side + i * 2)
+
+    loop(0, x, lower_row)
+    loop(0, y, lower_column)
+
     others = rows - local
-
-    def sub_ref(chunk, sub):
-        return qall.at[chunk, pl.ds(sub * sub_rows, sub_rows), :]
-
-    def member(offset):
-        return (g - 1 + 2 * members + offset) % members + 1
-
-    def ring(direction, step, sub):
-        sign = 1 - 2 * direction
-        ref = sub_ref(member(-sign * (step - 1)), sub)
+    near_first = sorted(range(1, side), key=lambda i: min(i, side - i))
+
+    def spread(delta, back=0, piece=None):
+        chunk = (g + side - back) % side
+        far = (delta + back) % side
+        n = rows if piece is None else rows // 2
+        ref = qall.at[chunk, pl.ds(0 if piece is None else piece * n, n), :]
+        slot = far if piece != 1 else 0
         return pltpu.make_async_remote_copy(
             src_ref=ref,
             dst_ref=ref,
-            send_sem=ring_send.at[direction, step - 1, sub],
-            recv_sem=ring_recv.at[direction, step - 1, sub],
-            device_id=line(a, member(sign), c),
+            send_sem=ring_send.at[slot],
+            recv_sem=ring_recv.at[slot],
+            device_id=line(a, (g + delta) % side, c),
             device_id_type=MESH,
         )
 
-    def ring_wait(direction, step, sub):
-        ref = sub_ref(member((2 * direction - 1) * step), sub)
-        pltpu.make_async_copy(ref, ref, ring_recv.at[direction, step - 1, sub]).wait()
-
-    def wait_own_queries():
-        own[0].wait()
-        ref = qall.at[0, pl.ds(0, others), :]
-        pltpu.make_async_copy(ref, ref, p1_recv.at[0]).wait()
-
-    @pl.when(g > 0)
-    def _():
-        wait_own_queries()
-        for step in range(1, steps + 2):
-            for sub in range(SUBS):
-                for direction in range(2):
-                    if step > 1:
-                        ring_wait(direction, step - 1, sub)
-                    if step <= steps:
-                        ring(direction, step, sub).start()
-
-    @pl.when((y == 0) & (me > 0))
-    def _():
-        hear(0)
-
-        @pl.when(x > 0)
-        def _():
-            hear(1)
-
-        push_row(0, 0)
-        push_row(1, 0)
-
-    @pl.when((x == 0) & (y > 0))
-    def _():
-        hear(2 * side)
-
-    def direct(chunk, to):
-        return pltpu.make_async_remote_copy(
-            src_ref=qall.at[chunk],
-            dst_ref=qall.at[chunk],
-            send_sem=direct_send.at[to],
-            recv_sem=direct_recv.at[chunk],
-            device_id=line(a, to, c),
-            device_id_type=MESH,
-        )
-
-    @pl.when(g > 0)
-    def _():
-        direct(g, 0).start()
-
-    far_first = sorted(range(1, side), key=lambda i: -min(i, side - i))
-
-    @pl.when(g == 0)
-    def _():
-        wait_own_queries()
-        for to in far_first:
-            direct(0, to).start()
+    def arrived(delta, piece=None):
+        chunk = (g + side - delta) % side
+        n = rows if piece is None else rows // 2
+        ref = qall.at[chunk, pl.ds(0 if piece is None else piece * n, n), :]
+        pltpu.make_async_copy(ref, ref, ring_recv.at[delta if piece != 1 else 0]).wait()
+
+    firsts = (1, side - 1, 2, side - 2)
+    first_hops = [spread(delta) for delta in firsts]
+    second_hops = {
+        2: [spread(1, 2), spread(2, 2, 0)],
+        side - 2: [spread(side - 1, side - 2), spread(side - 2, side - 2, 1)],
+    }
+
+    own[0].wait()
+    ref = qall.at[0, pl.ds(0, others), :]
+    pltpu.make_async_copy(ref, ref, p1_recv.at[0]).wait()
+    for copy in first_hops:
+        copy.start()
 
     for copy in own[1:]:
         copy.wait()
@@ -335,25 +284,31 @@
             device_id_type=MESH,
         )
 
-    def one_chunk(k):
-        chunk = side - 1 - k
-
-        @pl.when((g == 0) & (chunk > 0))
-        def _():
-            pltpu.make_async_copy(qall.at[chunk], qall.at[chunk], direct_recv.at[chunk]).wait()
-
-        @pl.when((g > 0) & (chunk == 0))
-        def _():
-            pltpu.make_async_copy(qall.at[0], qall.at[0], direct_recv.at[0]).wait()
-
+    def do_part(delta):
+        chunk = (g + side - delta) % side
         compute(chunk)
-
-        @pl.when(chunk != g)
-        def _():
-            part(0, chunk, g).start()
-            part(1, chunk, g).start()
-
-    loop(0, side, one_chunk)
+        part(0, chunk, g).start()
+        part(1, chunk, g).start()
+
+    def pass_on(delta):
+        arrived(delta)
+        for copy in second_hops[delta]:
+            copy.start()
+
+    compute(g)
+    for delta in (1, side - 1):
+        arrived(delta)
+        do_part(delta)
+    pass_on(2)
+    pass_on(side - 2)
+    do_part(2)
+    do_part(side - 2)
+    for delta in (3, side - 3):
+        arrived(delta)
+        do_part(delta)
+    arrived(half, 0)
+    arrived(half, 1)
+    do_part(half)
 
     orecv[g] = opart[g]
     lrecv[g] = lpart[g]
@@ -387,7 +342,7 @@
             device_id_type=MESH,
         ).start()
 
-    for j in far_first:
+    for j in sorted(range(1, side), key=lambda i: min(i, side - i)):
         for core in range(2):
             home((a + j) % side, core)
     home(a, 1 - c)
@@ -398,18 +353,8 @@
     ref = kv.at[:, pl.ds(0, others), :]
     pltpu.make_async_copy(ref, ref, p1_send.at[1]).wait()
 
-    @pl.when(g > 0)
-    def _():
-        for step in range(1, steps + 1):
-            for sub in range(SUBS):
-                for direction in range(2):
-                    ring(direction, step, sub).wait_send()
-        direct(g, 0).wait_send()
-
-    @pl.when(g == 0)
-    def _():
-        for to in far_first:
-            direct(0, to).wait_send()
+    for copy in first_hops + second_hops[2] + second_hops[side - 2]:
+        copy.wait_send()
 
     def part_left(chunk):
         @pl.when(chunk != g)
@@ -453,8 +398,6 @@
             dma((2,)),
             dma((2,)),
             pltpu.SemaphoreType.REGULAR((4 * side,)),
-            dma((2, half - 1, SUBS)),
-            dma((2, half - 1, SUBS)),
             dma((side,)),
             dma((side,)),
             dma((2, side)),

time: 71.2 us -> 62.6 us (0.88)
  Pallas kernels: 69.5 us -> 60.9 us
    pallas_call x1, Pallas kernels: 69.5 us -> 60.9 us  [shards(): pl.pallas_call(functools.partial(kernel, side, local), out_shape=jax.Shap...]
where the time goes in v4:
time: 62.6 us; the launch traced here: 62.5 us
  Pallas kernels  60.9 us (97%)
  local copies, waits for them, and re-layouts  1.57 us (3%)
    pallas_call x1, Pallas kernels, shards(): pl.pallas_call(functools.partial(kernel, side, local), out_shape=jax.Shap...  60.9 us
    unnamed x1, local copies, waits for them, and re-layouts  1.57 us

profile of v4, /device:TPU:513, one launch (start us, length us, event | category | flops | bytes accessed | tf_op | source)
XLA Modules:
  0.0 62.5 jit_solution(4045822924356854868)
XLA Ops:
  0.0 60.9 %shard_map.64 = bf16[32,2048]{1,0:T(8,128)(2,1)} custom-call(s32[4]{0:T(128)} %sizes.1, bf16[32,2048]{1,0:T(8,128)(2,1)} %q_in.1, bf16[32,2048]{1,0:T(8,128)(2,1)} %fk_in.1, bf16[32,2048]{1,0:T(8,128)(2,1)} %fv_in.1, bf16[32,2048]{1,0:T(8,128)(2,1)} %sk_in.1, bf16[32,2048]{1,0:T(8,128)(2,1)} %sv_in.1), custom_call_target="tpu_custom_call" | custom-call | tf_op jit(solution)/shard_map/pallas_call | solution.py:380
  60.9 1.6 %copy.8 = bf16[32,2048]{1,0:T(8,128)(2,1)} copy(bf16[32,2048]{1,0:T(8,128)(2,1)} %shard_map.64) | data formatting | bytes 262144

commit v5 on v4

--- a/solution.py
+++ b/solution.py
@@ -255,9 +255,9 @@
 
     eye = lax.broadcasted_iota(jnp.int32, (HEAD, HEAD), 0) == lax.broadcasted_iota(jnp.int32, (HEAD, HEAD), 1)
     contract = (((1,), (1,)), ((), ()))
-    def compute(chunk):
-        q = qall[chunk]
-        patch = patches(rows, 0, chunk)
+    def compute(chunk, first=0, count=rows):
+        q = qall[chunk, pl.ds(first, count), :]
+        patch = patches(count, first, chunk)
         split = jnp.concatenate([q * indicator(patch == p) for p in range(PATCHES)], axis=1)
         s = lax.dot_general(split, kcat[...], contract, preferred_element_type=jnp.float32)
         m = jnp.max(s, axis=1, keepdims=True)
@@ -267,19 +267,22 @@
         picked = o[:, :HEAD]
         for p in range(1, PATCHES):
             picked = jnp.where(patch == p, o[:, p * HEAD : (p + 1) * HEAD], picked)
-        opart[chunk] = (picked / total).astype(jnp.bfloat16)
+        opart[chunk, pl.ds(first, count), :] = (picked / total).astype(jnp.bfloat16)
         lse = m * scale2 + jnp.log2(total)
-        for k in range(rows // HEAD):
+        for k in range(count // HEAD):
             block_lse = lse[k * HEAD : (k + 1) * HEAD, :]
-            lpart[chunk, pl.ds(k, 1), :] = jnp.sum(jnp.where(eye, block_lse, 0.0), axis=0, keepdims=True)
-
-    def part(kind, chunk, source):
+            lpart[chunk, pl.ds(first // HEAD + k, 1), :] = jnp.sum(jnp.where(eye, block_lse, 0.0), axis=0, keepdims=True)
+
+    def part(kind, chunk, source, piece=None):
         src, dst = ((opart, orecv), (lpart, lrecv))[kind]
+        n = src.shape[1]
+        cut = pl.ds(0, n) if piece is None else pl.ds(piece * (n // 2), n // 2)
+        extra = piece == 1
         return pltpu.make_async_remote_copy(
-            src_ref=src.at[chunk],
-            dst_ref=dst.at[source],
-            send_sem=part_send.at[kind, chunk],
-            recv_sem=part_recv.at[kind, source],
+            src_ref=src.at[chunk, cut],
+            dst_ref=dst.at[source, cut],
+            send_sem=part_send.at[kind, side if extra else chunk],
+            recv_sem=part_recv.at[kind, side if extra else source],
             device_id=line(a, chunk, c),
             device_id_type=MESH,
         )
@@ -306,31 +309,30 @@
     for delta in (3, side - 3):
         arrived(delta)
         do_part(delta)
-    arrived(half, 0)
-    arrived(half, 1)
-    do_part(half)
+    opposite = (g + half) % side
+    halves = [(kind, piece) for piece in range(2) for kind in range(2)]
+    for piece in range(2):
+        arrived(half, piece)
+        compute(opposite, piece * (rows // 2), rows // 2)
+        for kind in range(2):
+            part(kind, opposite, g, piece).start()
 
     orecv[g] = opart[g]
     lrecv[g] = lpart[g]
 
-    def part_arrived(source):
-        @pl.when(source != g)
+    def part_arrived(delta):
+        source = (g + delta) % side
+
+        @pl.when(delta != half)
         def _():
             pltpu.make_async_copy(orecv.at[source], orecv.at[source], part_recv.at[0, source]).wait()
             pltpu.make_async_copy(lrecv.at[source], lrecv.at[source], part_recv.at[1, source]).wait()
 
-    loop(0, side, part_arrived)
-    lse = [lrecv[source] for source in range(side)]
-    top = functools.reduce(jnp.maximum, lse)
-    weights = [jnp.exp2(l - top) for l in lse]
-    total = functools.reduce(jnp.add, weights)
-    weights = [w / total for w in weights]
-    for t in range(rows // HEAD):
-        acc = jnp.zeros((HEAD, HEAD), jnp.float32)
-        for source in range(side):
-            w = jnp.sum(jnp.where(eye, weights[source][t : t + 1, :], 0.0), axis=1, keepdims=True)
-            acc = acc + w * orecv[source, pl.ds(t * HEAD, HEAD), :].astype(jnp.float32)
-        outst[pl.ds(t * HEAD, HEAD), :] = acc.astype(jnp.bfloat16)
+    def piece_arrived(piece):
+        for kind, ref in enumerate((orecv, lrecv)):
+            n = ref.shape[1] // 2
+            cut = ref.at[opposite, pl.ds(piece * n, n)]
+            pltpu.make_async_copy(cut, cut, part_recv.at[kind, side if piece else opposite]).wait()
 
     def home(a_to, core):
         pltpu.make_async_remote_copy(
@@ -342,11 +344,37 @@
             device_id_type=MESH,
         ).start()
 
-    for j in sorted(range(1, side), key=lambda i: min(i, side - i)):
-        for core in range(2):
-            home((a + j) % side, core)
-    home(a, 1 - c)
-    out[:, head_cols(own_head)] = outst[own_row, :]
+    def finish(piece):
+        n = rows // HEAD // 2
+        lse = [lrecv[source, pl.ds(piece * n, n)] for source in range(side)]
+        top = functools.reduce(jnp.maximum, lse)
+        weights = [jnp.exp2(l - top) for l in lse]
+        total = functools.reduce(jnp.add, weights)
+        weights = [w / total for w in weights]
+        for k in range(n):
+            tile = pl.ds((piece * n + k) * HEAD, HEAD)
+            acc = jnp.zeros((HEAD, HEAD), jnp.float32)
+            for source in range(side):
+                w = jnp.sum(jnp.where(eye, weights[source][k : k + 1, :], 0.0), axis=1, keepdims=True)
+                acc = acc + w * orecv[source, tile, :].astype(jnp.float32)
+            outst[tile, :] = acc.astype(jnp.bfloat16)
+        for j in near_first:
+            to = (a + j) % side
+
+            @pl.when(to // half == piece)
+            def _():
+                home(to, 0)
+                home(to, 1)
+
+        @pl.when(a // half == piece)
+        def _():
+            home(a, 1 - c)
+            out[:, head_cols(own_head)] = outst[own_row, :]
+
+    loop(1, side, part_arrived)
+    for piece in range(2):
+        piece_arrived(piece)
+        finish(piece)
 
     ref = qall.at[0, pl.ds(0, others), :]
     pltpu.make_async_copy(ref, ref, p1_send.at[0]).wait()
@@ -356,13 +384,17 @@
     for copy in first_hops + second_hops[2] + second_hops[side - 2]:
         copy.wait_send()
 
-    def part_left(chunk):
-        @pl.when(chunk != g)
+    def part_left(delta):
+        chunk = (g + delta) % side
+
+        @pl.when(delta != half)
         def _():
             part(0, chunk, g).wait_send()
             part(1, chunk, g).wait_send()
 
-    loop(0, side, part_left)
+    loop(1, side, part_left)
+    for kind, piece in halves:
+        part(kind, opposite, g, piece).wait_send()
     ref = outst.at[pl.ds(0, others), :]
     pltpu.make_async_copy(ref, ref, p4_recv).wait()
     pltpu.make_async_copy(ref, ref, p4_send).wait()
@@ -400,8 +432,8 @@
             pltpu.SemaphoreType.REGULAR((4 * side,)),
             dma((side,)),
             dma((side,)),
-            dma((2, side)),
-            dma((2, side)),
+            dma((2, side + 1)),
+            dma((2, side + 1)),
             dma,
             dma,
         ],

time: 62.6 us -> 61.7 us (0.986)
  Pallas kernels: 60.9 us -> 60 us
    pallas_call x1, Pallas kernels: 60.9 us -> 60 us  [shards(): pl.pallas_call(functools.partial(kernel, side, local), out_shape=jax.Shap...]
where the time goes in v5:
time: 61.7 us; the launch traced here: 61.6 us
  Pallas kernels  60 us (97%)
  local copies, waits for them, and re-layouts  1.57 us (3%)
    pallas_call x1, Pallas kernels, shards(): pl.pallas_call(functools.partial(kernel, side, local), out_shape=jax.Shap...  60 us
    unnamed x1, local copies, waits for them, and re-layouts  1.57 us

profile of v5, /device:TPU:513, one launch (start us, length us, event | category | flops | bytes accessed | tf_op | source)
XLA Modules:
  0.0 61.6 jit_solution(9553594075043767921)
XLA Ops:
  0.0 60.0 %shard_map.64 = bf16[32,2048]{1,0:T(8,128)(2,1)} custom-call(s32[4]{0:T(128)} %sizes.1, bf16[32,2048]{1,0:T(8,128)(2,1)} %q_in.1, bf16[32,2048]{1,0:T(8,128)(2,1)} %fk_in.1, bf16[32,2048]{1,0:T(8,128)(2,1)} %fv_in.1, bf16[32,2048]{1,0:T(8,128)(2,1)} %sk_in.1, bf16[32,2048]{1,0:T(8,128)(2,1)} %sv_in.1), custom_call_target="tpu_custom_call" | custom-call | tf_op jit(solution)/shard_map/pallas_call | solution.py:412
  60.0 1.6 %copy.8 = bf16[32,2048]{1,0:T(8,128)(2,1)} copy(bf16[32,2048]{1,0:T(8,128)(2,1)} %shard_map.64) | data formatting | bytes 262144

commit v6 on v5

--- a/solution.py
+++ b/solution.py
@@ -102,6 +102,27 @@
     def _():
         signal(barrier, at(x, y, 0))
 
+    higher = 2 * (side - 1 - x) + 2 * (side - 1 - y) + (1 - c)
+
+    @pl.when(higher > 0)
+    def _():
+        pl.semaphore_wait(barrier, higher)
+
+    def ready_row(i):
+        signal(ready.at[x * 2 + c], at(i, y, 0))
+        signal(ready.at[x * 2 + c], at(i, y, 1))
+
+    def ready_column(i):
+        signal(ready.at[2 * side + y * 2 + c], at(x, i, 0))
+        signal(ready.at[2 * side + y * 2 + c], at(x, i, 1))
+
+    loop(x + 1, side, ready_row)
+    loop(y + 1, side, ready_column)
+
+    @pl.when(c == 0)
+    def _():
+        signal(ready.at[x * 2], at(x, y, 1))
+
     own_row = block(a * 2 + c)
     own_head = c * side + a
     own = []
@@ -109,27 +130,6 @@
         dst = qall.at[g, own_row, :] if i == 0 else kv.at[i - 1, own_row, :]
         own.append(pltpu.make_async_copy(ref.at[:, head_cols(own_head)], dst, self_sem.at[i]))
         own[-1].start()
-
-    higher = 2 * (side - 1 - x) + 2 * (side - 1 - y) + (1 - c)
-
-    @pl.when(higher > 0)
-    def _():
-        pl.semaphore_wait(barrier, higher)
-
-    def ready_row(i):
-        signal(ready.at[x * 2 + c], at(i, y, 0))
-        signal(ready.at[x * 2 + c], at(i, y, 1))
-
-    def ready_column(i):
-        signal(ready.at[2 * side + y * 2 + c], at(x, i, 0))
-        signal(ready.at[2 * side + y * 2 + c], at(x, i, 1))
-
-    loop(x + 1, side, ready_row)
-    loop(y + 1, side, ready_column)
-
-    @pl.when(c == 0)
-    def _():
-        signal(ready.at[x * 2], at(x, y, 1))
 
     row_x, row_y = block(x * 2 + c), block(y * 2 + c)
 

time: 61.7 us -> 60.7 us (0.984)
  Pallas kernels: 60 us -> 58.6 us
    pallas_call x1, Pallas kernels: 60 us -> 58.6 us  [shards(): pl.pallas_call(functools.partial(kernel, side, local), out_shape=jax.Shap...]
where the time goes in v6:
time: 60.7 us; the launch traced here: 60.2 us
  Pallas kernels  58.6 us (97%)
  local copies, waits for them, and re-layouts  1.57 us (3%)
    pallas_call x1, Pallas kernels, shards(): pl.pallas_call(functools.partial(kernel, side, local), out_shape=jax.Shap...  58.6 us
    unnamed x1, local copies, waits for them, and re-layouts  1.57 us

profile of v6, /device:TPU:513, one launch (start us, length us, event | category | flops | bytes accessed | tf_op | source)
XLA Modules:
  0.0 60.2 jit_solution(8595703105186330162)
XLA Ops:
  0.0 58.6 %shard_map.64 = bf16[32,2048]{1,0:T(8,128)(2,1)} custom-call(s32[4]{0:T(128)} %sizes.1, bf16[32,2048]{1,0:T(8,128)(2,1)} %q_in.1, bf16[32,2048]{1,0:T(8,128)(2,1)} %fk_in.1, bf16[32,2048]{1,0:T(8,128)(2,1)} %fv_in.1, bf16[32,2048]{1,0:T(8,128)(2,1)} %sk_in.1, bf16[32,2048]{1,0:T(8,128)(2,1)} %sv_in.1), custom_call_target="tpu_custom_call" | custom-call | tf_op jit(solution)/shard_map/pallas_call | solution.py:412
  58.6 1.6 %copy.8 = bf16[32,2048]{1,0:T(8,128)(2,1)} copy(bf16[32,2048]{1,0:T(8,128)(2,1)} %shard_map.64) | data formatting | bytes 262144

commit v7 on v6

--- a/solution.py
+++ b/solution.py
@@ -69,8 +69,7 @@
 
     inputs = (q_in, fk_in, fv_in, sk_in, sv_in)
     loads = [pltpu.make_async_copy(ref, stage.at[i], load_sem.at[i]) for i, ref in enumerate(inputs)]
-    for copy in loads:
-        copy.start()
+    loads[0].start()
 
     def block(index):
         return pl.ds(pl.multiple_of(index * local, local), local)
@@ -122,6 +121,9 @@
     @pl.when(c == 0)
     def _():
         signal(ready.at[x * 2], at(x, y, 1))
+
+    for copy in loads[1:]:
+        copy.start()
 
     own_row = block(a * 2 + c)
     own_head = c * side + a

time: 60.7 us -> 62 us (1.021)
  Pallas kernels: 58.6 us -> 59.8 us
    pallas_call x1, Pallas kernels: 58.6 us -> 59.8 us  [shards(): pl.pallas_call(functools.partial(kernel, side, local), out_shape=jax.Shap...]
where the time goes in v7:
time: 62 us; the launch traced here: 61.3 us
  Pallas kernels  59.8 us (96%)
  local copies, waits for them, and re-layouts  1.57 us (3%)
    pallas_call x1, Pallas kernels, shards(): pl.pallas_call(functools.partial(kernel, side, local), out_shape=jax.Shap...  59.8 us
    unnamed x1, local copies, waits for them, and re-layouts  1.57 us

profile of v7, /device:TPU:513, one launch (start us, length us, event | category | flops | bytes accessed | tf_op | source)
XLA Modules:
  0.0 61.3 jit_solution(17036853574989203232)
XLA Ops:
  0.0 59.8 %shard_map.64 = bf16[32,2048]{1,0:T(8,128)(2,1)} custom-call(s32[4]{0:T(128)} %sizes.1, bf16[32,2048]{1,0:T(8,128)(2,1)} %q_in.1, bf16[32,2048]{1,0:T(8,128)(2,1)} %fk_in.1, bf16[32,2048]{1,0:T(8,128)(2,1)} %fv_in.1, bf16[32,2048]{1,0:T(8,128)(2,1)} %sk_in.1, bf16[32,2048]{1,0:T(8,128)(2,1)} %sv_in.1), custom_call_target="tpu_custom_call" | custom-call | tf_op jit(solution)/shard_map/pallas_call | solution.py:414
  59.8 1.6 %copy.8 = bf16[32,2048]{1,0:T(8,128)(2,1)} copy(bf16[32,2048]{1,0:T(8,128)(2,1)} %shard_map.64) | data formatting | bytes 262144
